TPU v7x, 32 devices: a whole 2x2x4 slice. The times are simulated.
32 devices in a mesh: seq: 8 (over y, x, core), chan: 4 (over z).
Axes of the slice: x: 2, y: 2, z: 4, core: 2. Of those that a mesh axis runs over, the one named last changes fastest.
Arguments:
- fwd_q: bfloat16 [1024, 4096], P('seq', 'chan'), may hold values from -6 to 6
- fwd_k: bfloat16 [1024, 4096], P('seq', 'chan'), may hold values from -6 to 6
- fwd_v: bfloat16 [1024, 4096], P('seq', 'chan'), may hold values from -6 to 6
- bwd_q: bfloat16 [1024, 4096], P('seq', 'chan'), may hold values from -6 to 6
- bwd_k: bfloat16 [1024, 4096], P('seq', 'chan'), may hold values from -6 to 6
- bwd_v: bfloat16 [1024, 4096], P('seq', 'chan'), may hold values from -6 to 6
- bwd_grad: bfloat16 [1024, 4096], P('seq', 'chan'), may hold values from -6 to 6
- filters: float32 [1024, 1024], P('seq', 'chan'), may hold values from -0.1875 to 0.1875
- skip: float32 [4096], P('chan'), may hold values from -4 to 4
Outputs:
- output: bfloat16 [1024, 4096], P('seq', 'chan')
- grad_query: bfloat16 [1024, 4096], P('seq', 'chan')
- grad_key: bfloat16 [1024, 4096], P('seq', 'chan')
- grad_value: bfloat16 [1024, 4096], P('seq', 'chan')
- grad_filter: float32 [1024, 1024], P('seq', 'chan')
- grad_skip: float32 [4096], P('chan')
All inputs are finite; a program needn't handle non-finite values.
Results may differ from a plain program's by a relative error of at most 0.0075.
Values may be sent and summed in bfloat16 or wider, within the bound.
A program may use at most 256 MiB of HBM per device.

v0:
```python
import functools
import math

import jax
import jax.numpy as jnp
import numpy as np
from jax import lax
from jax.experimental import pallas as pl
from jax.experimental.pallas import tpu as pltpu
from jax.sharding import PartitionSpec as P

HIGHEST = lax.Precision.HIGHEST
LANES = 128
MESH = pl.DeviceIdType.MESH
BF16 = jnp.bfloat16
F32 = jnp.float32


def index_ramp(total):
    return jnp.arange(total, dtype=jnp.int32)


def widened(values):
    return values.astype(jnp.float32)


def angles(out_index, in_index, period, sign):
    phase_steps = out_index[:, None] * in_index[None, :] % period
    phase = phase_steps.astype(jnp.float32) * (sign * 2.0 * math.pi / period)
    return (jnp.cos(phase), jnp.sin(phase))


def times_table(left, right):
    return (left[0] * right[0] - left[1] * right[1], left[0] * right[1] + left[1] * right[0])


def block_table(pair):
    cosine, sine_part = pair
    return jnp.stack([jnp.stack([cosine, -sine_part]), jnp.stack([sine_part, cosine])])


def product_of(left, right):
    return jnp.stack(
        [left[0] * right[0] - left[1] * right[1], left[0] * right[1] + left[1] * right[0]]
    )


def conj_product(left, right):
    return jnp.stack(
        [left[0] * right[0] + left[1] * right[1], left[0] * right[1] - left[1] * right[0]]
    )


def joined(left, right):
    return jnp.concatenate([left, right], axis=-1)


def factor(total):
    chosen = 1
    for candidate in range(1, total + 1):
        if candidate * candidate <= total and total % candidate == 0:
            chosen = candidate
    return chosen


def leading_section(values, seq_size):
    cosine, sine_part = angles(index_ramp(2 * seq_size), index_ramp(seq_size), 2 * seq_size, -1.0)
    table = jnp.stack([cosine, sine_part])
    return jnp.einsum("rkp,pmc->rkmc", table, values, precision=HIGHEST)


def trailing_section(values, seq_size, period):
    cosine, sine_part = angles(index_ramp(seq_size), index_ramp(2 * seq_size), 2 * seq_size, 1.0)
    table = jnp.stack([cosine, -sine_part]) * (1.0 / period)
    return jnp.einsum("rpk,rkmc->pmc", table, values, precision=HIGHEST)


def inner_forward(values, freq_keys, period):
    lead_size, row_count, chan_count = values.shape[1:]
    outer_size = factor(row_count)
    inner_size = row_count // outer_size
    values = values.reshape(2, lead_size, outer_size, inner_size, chan_count)
    first_twiddle = angles(freq_keys, index_ramp(row_count), period, -1.0)
    first_twiddle = tuple(
        (part.reshape(lead_size, outer_size, inner_size) for part in first_twiddle)
    )
    outer_dft = angles(index_ramp(outer_size), index_ramp(outer_size), outer_size, -1.0)
    outer_table = times_table(
        tuple((part[None, :, :, None] for part in outer_dft)),
        tuple((part[:, None, :, :] for part in first_twiddle)),
    )
    values = jnp.einsum("rsjxab,sjabc->rjxbc", block_table(outer_table), values, precision=HIGHEST)
    second_twiddle = angles(index_ramp(outer_size), index_ramp(inner_size), row_count, -1.0)
    inner_dft = angles(index_ramp(inner_size), index_ramp(inner_size), inner_size, -1.0)
    inner_table = times_table(
        tuple((part[None, :, :] for part in inner_dft)),
        tuple((part[:, None, :] for part in second_twiddle)),
    )
    return jnp.einsum("rsxyb,sjxbc->rjxyc", block_table(inner_table), values, precision=HIGHEST)


def inner_inverse(values, freq_keys, period):
    lead_size, outer_size, inner_size, chan_count = values.shape[1:]
    row_count = outer_size * inner_size
    second_twiddle = angles(index_ramp(outer_size), index_ramp(inner_size), row_count, 1.0)
    inner_dft = angles(index_ramp(inner_size), index_ramp(inner_size), inner_size, 1.0)
    inner_table = times_table(
        tuple((part[:, :, None] for part in second_twiddle)),
        tuple((part[None, :, :] for part in inner_dft)),
    )
    values = jnp.einsum("rsxby,sjxyc->rjxbc", block_table(inner_table), values, precision=HIGHEST)
    first_twiddle = angles(freq_keys, index_ramp(row_count), period, 1.0)
    first_twiddle = tuple(
        (part.reshape(lead_size, outer_size, inner_size) for part in first_twiddle)
    )
    outer_dft = angles(index_ramp(outer_size), index_ramp(outer_size), outer_size, 1.0)
    outer_table = times_table(
        tuple((part[:, :, :, None] for part in first_twiddle)),
        tuple((part[None, :, None, :] for part in outer_dft)),
    )
    values = jnp.einsum("rsjabx,sjxbc->rjabc", block_table(outer_table), values, precision=HIGHEST)
    return values.reshape(2, lead_size, row_count, chan_count)


def forward_local(signal_part, seq_size):
    seq_length, chan_count = signal_part.shape
    row_count = seq_length // seq_size
    values = leading_section(signal_part.reshape(seq_size, row_count, chan_count), seq_size)
    return inner_forward(values, index_ramp(2 * seq_size), 2 * seq_length)


def inverse_local(values, seq_size):
    lead_size, outer_size, inner_size, chan_count = values.shape[1:]
    row_count = outer_size * inner_size
    period = 2 * seq_size * row_count
    values = inner_inverse(values, index_ramp(2 * seq_size), period)
    return trailing_section(values, seq_size, period).reshape(seq_size * row_count, chan_count)


def filter_times_pair(spec_filter, spec_pair):
    shape_pair = spec_pair.shape
    width = spec_filter.shape[-1]
    pair_view = spec_pair.reshape(shape_pair[:-1] + (2, width))
    filter_view = spec_filter[..., None, :]
    return product_of(filter_view, pair_view).reshape(shape_pair)


def per_device(fwd_q, fwd_k, fwd_v, bwd_q, bwd_k, bwd_v, bwd_grad, filters, skip):
    row_count, chan_width = fwd_q.shape
    seq_size = lax.axis_size("seq")
    grad_scale = 1.0 / math.sqrt(row_count * seq_size)
    source = (widened(fwd_k) * widened(fwd_v)).astype(jnp.bfloat16)
    second_source = (widened(bwd_k) * widened(bwd_v)).astype(jnp.bfloat16)
    upstream = (widened(bwd_grad) * widened(bwd_q)).astype(jnp.bfloat16)
    skip_gain = widened(skip)
    filters_all = lax.all_gather(filters, "chan", axis=1, tiled=True)
    narrow = chan_width // seq_size
    local_first, local_second = (
        lax.all_to_all(source, "seq", split_axis=1, concat_axis=0, tiled=True),
        lax.all_to_all(second_source, "seq", split_axis=1, concat_axis=0, tiled=True),
    )
    local_filter = lax.all_to_all(filters_all, "seq", split_axis=1, concat_axis=0, tiled=True)
    local_up = lax.all_to_all(upstream, "seq", split_axis=1, concat_axis=0, tiled=True)
    spec_sources = forward_local(
        widened(jnp.concatenate([local_first, local_second], axis=1)), seq_size
    )
    spec_filter = forward_local(local_filter, seq_size)
    conv_local = inverse_local(filter_times_pair(spec_filter, spec_sources), seq_size)
    conv_first, conv_second = (
        lax.all_to_all(conv_local[:, :narrow], "seq", split_axis=0, concat_axis=1, tiled=True),
        lax.all_to_all(conv_local[:, narrow:], "seq", split_axis=0, concat_axis=1, tiled=True),
    )
    spec_up = forward_local(widened(local_up), seq_size)
    spec_second = spec_sources[..., narrow:]
    back_local = inverse_local(
        joined(conj_product(spec_filter, spec_up), conj_product(spec_second, spec_up)), seq_size
    )
    through_conv, filter_terms = (
        lax.all_to_all(back_local[:, :narrow], "seq", split_axis=0, concat_axis=1, tiled=True),
        lax.all_to_all(
            back_local[:, narrow:] * grad_scale, "seq", split_axis=0, concat_axis=1, tiled=True
        ),
    )
    grad_filter = lax.psum_scatter(filter_terms, "chan", scatter_dimension=1, tiled=True)
    source_wide = widened(source)
    second_wide = widened(second_source)
    upstream_wide = widened(upstream)
    mixed = conv_first + skip_gain * source_wide
    output = (widened(fwd_q) * mixed).astype(jnp.bfloat16)
    mixed_two = conv_second + skip_gain * second_wide
    grad_query = (widened(bwd_grad) * mixed_two).astype(jnp.bfloat16)
    through = through_conv + skip_gain * upstream_wide
    grad_key = (through * widened(bwd_v)).astype(jnp.bfloat16)
    grad_value = (through * widened(bwd_k)).astype(jnp.bfloat16)
    grad_skip = lax.psum(jnp.sum(upstream_wide * second_wide, axis=0) * grad_scale, "seq")
    return (output, grad_query, grad_key, grad_value, grad_filter, grad_skip)


def block_tables(rows):
    freq = 2 * np.arange(rows)[:, None] + 1
    phase = (freq * np.arange(rows)[None, :] % (4 * rows)) * (np.pi / (2 * rows))
    forward = np.concatenate([np.cos(phase), -np.sin(phase)], axis=0)
    inverse = np.concatenate([np.cos(phase), -np.sin(phase)], axis=0).T / rows
    return forward.astype(np.float32), inverse.astype(np.float32)


def kernel(
    n, nc, scale,
    fq, fk, fv, bq, bk, bv, bg, filt, skip, fwd_t, inv_t,
    out_o, gq_o, gk_o, gv_o, gf_o, gs_o,
    su_send, s1_send, fz, su, s1, rf, spec_s, spec_u, spec_f, spec_w, prod,
    c_send, c_recv, g_send, rg, zg, k_send, k_recv,
    su_ss, su_rs, s1_ss, s1_rs, f_ss, f_rs, z_ss, z_rs, c_ss, c_rs, g_ss, g_rs, y_ss, y_rs, k_ss, k_rs,
):
    rows, chan_width = fq.shape
    w = chan_width // n
    per = filt.shape[1] // w
    me = lax.axis_index("seq")
    mz = lax.axis_index("chan")
    peers = [lax.rem(me + r, n) for r in range(1, n)]
    zpeers = [lax.rem(mz + r, nc) for r in range(1, nc)]
    started = []

    def lane(p):
        return pl.ds(pl.multiple_of(p * w, w), w)

    def copy(src, dst, ss, rs, to):
        return pltpu.make_async_remote_copy(
            src_ref=src, dst_ref=dst, send_sem=ss, recv_sem=rs, device_id=to, device_id_type=MESH
        )

    def send(src, dst, ss, rs, to):
        c = copy(src, dst, ss, rs, to)
        c.start()
        started.append(c)

    def arrived(buf, ss, rs, to):
        copy(buf, buf, ss, rs, to).wait_recv()

    barrier = pltpu.get_barrier_semaphore()
    for p in peers:
        pl.semaphore_signal(barrier, inc=1, device_id={"seq": p}, device_id_type=MESH)
    for z in zpeers:
        pl.semaphore_signal(barrier, inc=1, device_id={"chan": z}, device_id_type=MESH)

    for h in range(per):
        fz[mz * per + h] = filt[:, h * w:(h + 1) * w].astype(BF16)
    for p in range(n):
        cols = slice(p * w, (p + 1) * w)
        su_send[p, 0] = (bk[:, cols].astype(F32) * bv[:, cols].astype(F32)).astype(BF16)
        su_send[p, 1] = (bg[:, cols].astype(F32) * bq[:, cols].astype(F32)).astype(BF16)
    pl.semaphore_wait(barrier, n - 1 + nc - 1)

    for z in zpeers:
        part = fz.at[pl.ds(mz * per, per)]
        send(part, part, z_ss.at[z], z_rs.at[mz], {"chan": z})
    for p in peers:
        send(su_send.at[p], su.at[me], su_ss.at[p], su_rs.at[me], {"seq": p})
    for p in range(n):
        cols = slice(p * w, (p + 1) * w)
        s1_send[p] = (fk[:, cols].astype(F32) * fv[:, cols].astype(F32)).astype(BF16)
    for z in zpeers:
        arrived(fz.at[pl.ds(z * per, per)], z_ss.at[z], z_rs.at[z], {"chan": z})
    for p in peers:
        send(fz.at[p], rf.at[me], f_ss.at[p], f_rs.at[me], {"seq": p})
    for p in peers:
        send(s1_send.at[p], s1.at[me], s1_ss.at[p], s1_rs.at[me], {"seq": p})
    su[me] = su_send[me]
    s1[me] = s1_send[me]
    rf[me] = fz[me]

    def transform(dst, q, block):
        dst[q] = jnp.dot(fwd_t[...], block, preferred_element_type=F32)

    sign = 1.0 - 2.0 * lax.rem(lax.broadcasted_iota(jnp.int32, (rows, w), 0), 2).astype(F32)

    def windowed(src):
        spec_w[0] = src[0]
        for d in range(1, n):
            spec_w[d, :rows] = src[d, :rows] - sign * src[d - 1, rows:]
            spec_w[d, rows:] = src[d, rows:] + sign * src[d - 1, :rows]

    def products(src, corr):
        def tile(k, carry):
            re_at = pl.ds(pl.multiple_of(k * 8, 8), 8)
            im_at = pl.ds(pl.multiple_of(rows + k * 8, 8), 8)
            ar = [spec_w[d, re_at] for d in range(n)]
            ai = [spec_w[d, im_at] for d in range(n)]
            xr = [src[d, re_at] for d in range(n)]
            xi = [src[d, im_at] for d in range(n)]
            for b in range(n):
                terms = [(c - b, c) for c in range(b, n)] if corr else [(b - c, c) for c in range(b + 1)]
                re, im = None, None
                for d, c in terms:
                    if corr:
                        tr = ar[d] * xr[c] + ai[d] * xi[c]
                        ti = ar[d] * xi[c] - ai[d] * xr[c]
                    else:
                        tr = ar[d] * xr[c] - ai[d] * xi[c]
                        ti = ar[d] * xi[c] + ai[d] * xr[c]
                    re = tr if re is None else re + tr
                    im = ti if im is None else im + ti
                prod[b, re_at] = re
                prod[b, im_at] = im
            return carry

        lax.fori_loop(0, rows // 8, tile, 0)

    def inverse(b):
        return jnp.dot(inv_t[...], prod[b].astype(BF16), preferred_element_type=F32)

    def give_back(which):
        for b in range(n):
            c_send[which, b] = inverse(b).astype(BF16)
        for p in peers:
            send(c_send.at[which, p], c_recv.at[which, me], c_ss.at[which, p], c_rs.at[which, me], {"seq": p})
        c_recv[which, me] = c_send[which, me]

    total = jnp.zeros((1, w), F32)
    for q in [me] + peers:
        if q is not me:
            arrived(su.at[q], su_ss.at[q], su_rs.at[q], {"seq": q})
        transform(spec_s, q, su[q, 0])
        transform(spec_u, q, su[q, 1])
        total += jnp.sum(su[q, 0].astype(F32) * su[q, 1].astype(F32), axis=0, keepdims=True)
    k_send[...] = jnp.broadcast_to(total * scale, k_send.shape)
    for p in peers:
        send(k_send, k_recv.at[me], k_ss.at[p], k_rs.at[me], {"seq": p})
    k_recv[me] = k_send[...]

    windowed(spec_s)
    products(spec_u, True)
    for b in range(n):
        g_send[b] = (inverse(b) * scale).astype(BF16)
    for p in peers:
        send(g_send.at[p], rg.at[me], g_ss.at[p], g_rs.at[me], {"seq": p})
    rg[me] = g_send[me]

    for q in [me] + peers:
        if q is not me:
            arrived(rf.at[q], f_ss.at[q], f_rs.at[q], {"seq": q})
        transform(spec_f, q, rf[q])
    windowed(spec_f)
    products(spec_s, False)
    give_back(0)
    products(spec_u, True)
    give_back(1)

    for q in [me] + peers:
        if q is not me:
            arrived(s1.at[q], s1_ss.at[q], s1_rs.at[q], {"seq": q})
        transform(spec_s, q, s1[q])
    products(spec_s, False)
    give_back(2)

    for q in peers:
        arrived(rg.at[q], g_ss.at[q], g_rs.at[q], {"seq": q})
    for z in zpeers:
        send(rg.at[pl.ds(z * per, per)], zg.at[mz], y_ss.at[z], y_rs.at[mz], {"chan": z})

    for q in [me] + peers:
        at = lane(q)
        gain = skip[:, at]
        if q is not me:
            arrived(c_recv.at[0, q], c_ss.at[0, q], c_rs.at[0, q], {"seq": q})
        mixed = c_recv[0, q].astype(F32) + gain * su_send[q, 0].astype(F32)
        gq_o[:, at] = (bg[:, at].astype(F32) * mixed).astype(BF16)
    for q in [me] + peers:
        at = lane(q)
        gain = skip[:, at]
        if q is not me:
            arrived(c_recv.at[1, q], c_ss.at[1, q], c_rs.at[1, q], {"seq": q})
        through = c_recv[1, q].astype(F32) + gain * su_send[q, 1].astype(F32)
        gk_o[:, at] = (through * bv[:, at].astype(F32)).astype(BF16)
        gv_o[:, at] = (through * bk[:, at].astype(F32)).astype(BF16)
    for z in zpeers:
        arrived(zg.at[z], y_ss.at[z], y_rs.at[z], {"chan": z})
    for h in range(per):
        acc = rg[mz * per + h].astype(F32)
        for z in zpeers:
            acc += zg[z, h].astype(F32)
        gf_o[:, h * w:(h + 1) * w] = acc
    for q in peers:
        arrived(k_recv.at[q], k_ss.at[q], k_rs.at[q], {"seq": q})
    for q in range(n):
        gs_o[:, q * w:(q + 1) * w] = k_recv[q, 0:1]
    for q in [me] + peers:
        at = lane(q)
        gain = skip[:, at]
        if q is not me:
            arrived(c_recv.at[2, q], c_ss.at[2, q], c_rs.at[2, q], {"seq": q})
        mixed = c_recv[2, q].astype(F32) + gain * s1_send[q].astype(F32)
        out_o[:, at] = (fq[:, at].astype(F32) * mixed).astype(BF16)
    for c in started:
        c.wait_send()


def fused_device(n, nc, *args):
    fwd_q, filters, skip = args[0], args[7], args[8]
    rows, chan_width = fwd_q.shape
    w = chan_width // n
    per = filters.shape[1] // w
    scale = 1.0 / math.sqrt(rows * n)
    forward, inverse = (jnp.asarray(t, dtype=BF16) for t in block_tables(rows))
    wide = jax.ShapeDtypeStruct((rows, chan_width), BF16)
    vmem = pl.BlockSpec(memory_space=pltpu.VMEM)
    dma = pltpu.SemaphoreType.DMA
    block = (n, rows, w)
    spectrum = (n, 2 * rows, w)
    scratch = [
        pltpu.VMEM((n, 2, rows, w), BF16), pltpu.VMEM(block, BF16), pltpu.VMEM(block, BF16),
        pltpu.VMEM((n, 2, rows, w), BF16), pltpu.VMEM(block, BF16), pltpu.VMEM(block, BF16),
        *[pltpu.VMEM(spectrum, F32)] * 5,
        pltpu.VMEM((3,) + block, BF16), pltpu.VMEM((3,) + block, BF16),
        pltpu.VMEM(block, BF16), pltpu.VMEM(block, BF16), pltpu.VMEM((nc, per, rows, w), BF16),
        pltpu.VMEM((8, w), F32), pltpu.VMEM((n, 8, w), F32),
        dma((n,)), dma((n,)), dma((n,)), dma((n,)), dma((n,)), dma((n,)), dma((nc,)), dma((nc,)),
        dma((3, n)), dma((3, n)), dma((n,)), dma((n,)), dma((nc,)), dma((nc,)), dma((n,)), dma((n,)),
    ]
    outs = pl.pallas_call(
        functools.partial(kernel, n, nc, scale),
        out_shape=(
            wide, wide, wide, wide,
            jax.ShapeDtypeStruct(filters.shape, F32), jax.ShapeDtypeStruct((1, chan_width), F32),
        ),
        in_specs=[vmem] * 11,
        out_specs=(vmem,) * 6,
        scratch_shapes=scratch,
        compiler_params=pltpu.CompilerParams(
            collective_id=0, has_side_effects=True, vmem_limit_bytes=48 * 1024 * 1024
        ),
    )(*args[:8], skip.reshape(1, chan_width), forward, inverse)
    return outs[:5] + (outs[5].reshape(chan_width),)


def routed(*args):
    n, nc = lax.axis_size("seq"), lax.axis_size("chan")
    rows, chan_width = args[0].shape
    filter_width = args[7].shape[1]
    fits = chan_width % (n * LANES) == 0 and rows % 16 == 0
    if fits and filter_width * nc == chan_width and filter_width % (chan_width // n) == 0:
        return fused_device(n, nc, *args)
    return per_device(*args)


def solution(mesh):
    return jax.shard_map(
        routed,
        mesh=mesh,
        in_specs=(
            P("seq", "chan"),
            P("seq", "chan"),
            P("seq", "chan"),
            P("seq", "chan"),
            P("seq", "chan"),
            P("seq", "chan"),
            P("seq", "chan"),
            P("seq", "chan"),
            P("chan"),
        ),
        out_specs=(
            P("seq", "chan"),
            P("seq", "chan"),
            P("seq", "chan"),
            P("seq", "chan"),
            P("seq", "chan"),
            P("chan"),
        ),
        check_vma=False,
    )
```

profile of v0, /device:TPU:0, one launch (start us, length us, event | category | flops | bytes accessed | tf_op | source)
XLA Modules:
  0.0 45.9 jit_solution(1524204952790265389)
XLA Ops:
  0.6 0.0 copy-start
  0.6 0.9 %copy-done = bf16[128,1024]{1,0:T(8,128)(2,1)S(1)} copy-done((bf16[128,1024]{1,0:T(8,128)(2,1)S(1)}, bf16[128,1024]{1,0:T(8,128)(2,1)}, u32[]{:S(2)}) %copy-start) | copy-done | bytes 262168
  1.6 0.0 copy-start.1
  1.6 0.9 %copy-done.1 = bf16[128,1024]{1,0:T(8,128)(2,1)S(1)} copy-done((bf16[128,1024]{1,0:T(8,128)(2,1)S(1)}, bf16[128,1024]{1,0:T(8,128)(2,1)}, u32[]{:S(2)}) %copy-start.1) | copy-done | bytes 262168
  2.5 0.0 copy-start.2
  2.5 0.9 %copy-done.2 = bf16[128,1024]{1,0:T(8,128)(2,1)S(1)} copy-done((bf16[128,1024]{1,0:T(8,128)(2,1)S(1)}, bf16[128,1024]{1,0:T(8,128)(2,1)}, u32[]{:S(2)}) %copy-start.2) | copy-done | bytes 262168
  3.5 0.0 copy-start.3
  3.5 0.9 %copy-done.3 = bf16[128,1024]{1,0:T(8,128)(2,1)S(1)} copy-done((bf16[128,1024]{1,0:T(8,128)(2,1)S(1)}, bf16[128,1024]{1,0:T(8,128)(2,1)}, u32[]{:S(2)}) %copy-start.3) | copy-done | bytes 262168
  4.4 0.0 copy-start.4
  4.4 0.9 %copy-done.4 = bf16[128,1024]{1,0:T(8,128)(2,1)S(1)} copy-done((bf16[128,1024]{1,0:T(8,128)(2,1)S(1)}, bf16[128,1024]{1,0:T(8,128)(2,1)}, u32[]{:S(2)}) %copy-start.4) | copy-done | bytes 262168
  5.4 0.0 copy-start.5
  5.4 0.9 %copy-done.5 = bf16[128,1024]{1,0:T(8,128)(2,1)S(1)} copy-done((bf16[128,1024]{1,0:T(8,128)(2,1)S(1)}, bf16[128,1024]{1,0:T(8,128)(2,1)}, u32[]{:S(2)}) %copy-start.5) | copy-done | bytes 262168
  6.3 0.0 copy-start.6
  6.3 0.9 %copy-done.6 = bf16[128,1024]{1,0:T(8,128)(2,1)S(1)} copy-done((bf16[128,1024]{1,0:T(8,128)(2,1)S(1)}, bf16[128,1024]{1,0:T(8,128)(2,1)}, u32[]{:S(2)}) %copy-start.6) | copy-done | bytes 262168
  7.3 0.0 copy-start.7
  7.3 0.9 %copy-done.7 = f32[128,256]{1,0:T(8,128)S(1)} copy-done((f32[128,256]{1,0:T(8,128)S(1)}, f32[128,256]{1,0:T(8,128)}, u32[]{:S(2)}) %copy-start.7) | copy-done | bytes 131096
  8.2 0.0 copy-start.8
  8.2 0.8 %copy-done.8 = bf16[128,256]{1,0:T(8,128)(2,1)S(1)} copy-done((bf16[128,256]{1,0:T(8,128)(2,1)S(1)}, bf16[128,256]{1,0:T(8,128)(2,1)}, u32[]{:S(2)}) %copy-start.8) | copy-done | bytes 65560
  9.0 0.0 copy-start.9
  9.0 0.8 %copy-done.9 = bf16[256,128]{1,0:T(8,128)(2,1)S(1)} copy-done((bf16[256,128]{1,0:T(8,128)(2,1)S(1)}, bf16[256,128]{1,0:T(8,128)(2,1)}, u32[]{:S(2)}) %copy-start.9) | copy-done | bytes 65560
  9.9 0.0 copy-start.10
  9.9 0.7 %copy-done.10 = f32[1024]{0:T(1024)S(1)} copy-done((f32[1024]{0:T(1024)S(1)}, f32[1024]{0:T(1024)}, u32[]{:S(2)}) %copy-start.10) | copy-done | bytes 4120
  10.6 31.2 %shard_map.154 = (bf16[128,1024]{1,0:T(8,128)(2,1)S(1)}, bf16[128,1024]{1,0:T(8,128)(2,1)S(1)}, bf16[128,1024]{1,0:T(8,128)(2,1)S(1)}, bf16[128,1024]{1,0:T(8,12...) custom-call(bf16[128,1024]{1,0:T(8,128)(2,1)S(1)} %copy-done, bf16[128,1024]{1,0:T(8,128)(2,1)S(1)} %copy-done.1, ...), custom_call_target="tpu_custom_call" | custom-call | tf_op jit(solution)/shard_map/pallas_call | solution.py:420
  41.8 0.7 %copy.23 = bf16[128,1024]{1,0:T(8,128)(2,1)} copy(bf16[128,1024]{1,0:T(8,128)(2,1)S(1)} %get-tuple-element.24) | data formatting | bytes 524288
  42.5 0.7 %copy.24 = bf16[128,1024]{1,0:T(8,128)(2,1)} copy(bf16[128,1024]{1,0:T(8,128)(2,1)S(1)} %get-tuple-element.25) | data formatting | bytes 524288
  43.2 0.7 %copy.25 = bf16[128,1024]{1,0:T(8,128)(2,1)} copy(bf16[128,1024]{1,0:T(8,128)(2,1)S(1)} %get-tuple-element.26) | data formatting | bytes 524288
  43.9 0.7 %copy.26 = bf16[128,1024]{1,0:T(8,128)(2,1)} copy(bf16[128,1024]{1,0:T(8,128)(2,1)S(1)} %get-tuple-element.27) | data formatting | bytes 524288
  44.6 0.7 %copy.27 = f32[128,256]{1,0:T(8,128)} copy(f32[128,256]{1,0:T(8,128)S(1)} %get-tuple-element.28) | data formatting | bytes 262144
  45.3 0.6 %copy.28 = f32[1024]{0:T(1024)} copy(f32[1024]{0:T(1024)S(1)} %bitcast.3) | data formatting | bytes 8192
Async XLA Ops:
  0.6 1.0 %copy-start = (bf16[128,1024]{1,0:T(8,128)(2,1)S(1)}, bf16[128,1024]{1,0:T(8,128)(2,1)}, u32[]{:S(2)}) copy-start(bf16[128,1024]{1,0:T(8,128)(2,1)} %fq.1) | copy-start | bytes 786436
  1.6 0.9 %copy-start.1 = (bf16[128,1024]{1,0:T(8,128)(2,1)S(1)}, bf16[128,1024]{1,0:T(8,128)(2,1)}, u32[]{:S(2)}) copy-start(bf16[128,1024]{1,0:T(8,128)(2,1)} %fk.1) | copy-start | bytes 786436
  2.5 0.9 %copy-start.2 = (bf16[128,1024]{1,0:T(8,128)(2,1)S(1)}, bf16[128,1024]{1,0:T(8,128)(2,1)}, u32[]{:S(2)}) copy-start(bf16[128,1024]{1,0:T(8,128)(2,1)} %fv.1) | copy-start | bytes 786436
  3.5 0.9 %copy-start.3 = (bf16[128,1024]{1,0:T(8,128)(2,1)S(1)}, bf16[128,1024]{1,0:T(8,128)(2,1)}, u32[]{:S(2)}) copy-start(bf16[128,1024]{1,0:T(8,128)(2,1)} %bq.1) | copy-start | bytes 786436
  4.4 0.9 %copy-start.4 = (bf16[128,1024]{1,0:T(8,128)(2,1)S(1)}, bf16[128,1024]{1,0:T(8,128)(2,1)}, u32[]{:S(2)}) copy-start(bf16[128,1024]{1,0:T(8,128)(2,1)} %bk.1) | copy-start | bytes 786436
  5.4 0.9 %copy-start.5 = (bf16[128,1024]{1,0:T(8,128)(2,1)S(1)}, bf16[128,1024]{1,0:T(8,128)(2,1)}, u32[]{:S(2)}) copy-start(bf16[128,1024]{1,0:T(8,128)(2,1)} %bv.1) | copy-start | bytes 786436
  6.3 0.9 %copy-start.6 = (bf16[128,1024]{1,0:T(8,128)(2,1)S(1)}, bf16[128,1024]{1,0:T(8,128)(2,1)}, u32[]{:S(2)}) copy-start(bf16[128,1024]{1,0:T(8,128)(2,1)} %bg.1) | copy-start | bytes 786436
  7.3 0.9 %copy-start.7 = (f32[128,256]{1,0:T(8,128)S(1)}, f32[128,256]{1,0:T(8,128)}, u32[]{:S(2)}) copy-start(f32[128,256]{1,0:T(8,128)} %filt.1) | copy-start | bytes 393220
  8.2 0.8 %copy-start.8 = (bf16[128,256]{1,0:T(8,128)(2,1)S(1)}, bf16[128,256]{1,0:T(8,128)(2,1)}, u32[]{:S(2)}) copy-start(bf16[128,256]{1,0:T(8,128)(2,1)} %constant.5.clone.inv_t) | copy-start | bytes 196612
  9.0 0.8 %copy-start.9 = (bf16[256,128]{1,0:T(8,128)(2,1)S(1)}, bf16[256,128]{1,0:T(8,128)(2,1)}, u32[]{:S(2)}) copy-start(bf16[256,128]{1,0:T(8,128)(2,1)} %constant.4.clone.fwd_t) | copy-start | bytes 196612
  9.9 0.7 %copy-start.10 = (f32[1024]{0:T(1024)S(1)}, f32[1024]{0:T(1024)}, u32[]{:S(2)}) copy-start(f32[1024]{0:T(1024)} %param.19) | copy-start | bytes 12292
where the time goes:
time: 46.3 us; the launch traced here: 45.9 us
  Pallas kernels  31.2 us (67%)
  local copies, waits for them, and re-layouts  14 us (30%)
  between operations  0.66 us (1%)
    pallas_call x1, Pallas kernels, fused_device(): pl.pallas_call(functools.partial(kernel, n, nc, scale), out_shape=(wide,...  31.2 us
    unnamed x28, local copies, waits for them, and re-layouts  14 us

commit v1 on v0

--- a/solution.py
+++ b/solution.py
@@ -206,8 +206,10 @@
 
 def kernel(
     n, nc, scale,
-    fq, fk, fv, bq, bk, bv, bg, filt, skip, fwd_t, inv_t,
-    out_o, gq_o, gk_o, gv_o, gf_o, gs_o,
+    fq_h, fk_h, fv_h, bq_h, bk_h, bv_h, bg_h, filt_h, skip_h, fwd_h, inv_h,
+    out_h, gq_h, gk_h, gv_h, gf_h, gs_h,
+    fq, fk, fv, bq, bk, bv, bg, filt, skip, fwd_t, inv_t, in_sem,
+    out_o, gq_o, gk_o, gv_o, gf_o, gs_o, out_sem,
     su_send, s1_send, fz, su, s1, rf, spec_s, spec_u, spec_f, spec_w, prod,
     c_send, c_recv, g_send, rg, zg, k_send, k_recv,
     su_ss, su_rs, s1_ss, s1_rs, f_ss, f_rs, z_ss, z_rs, c_ss, c_rs, g_ss, g_rs, y_ss, y_rs, k_ss, k_rs,
@@ -237,36 +239,59 @@
     def arrived(buf, ss, rs, to):
         copy(buf, buf, ss, rs, to).wait_recv()
 
+    loads = {}
+    order = ((filt_h, filt), (bk_h, bk), (bv_h, bv), (bg_h, bg), (bq_h, bq), (fk_h, fk), (fv_h, fv))
+    for at, (far, near) in enumerate(order + ((fwd_h, fwd_t), (inv_h, inv_t), (skip_h, skip), (fq_h, fq))):
+        loads[id(near)] = pltpu.make_async_copy(far, near, in_sem.at[at])
+        loads[id(near)].start()
+
+    def loaded(*refs):
+        for ref in refs:
+            loads[id(ref)].wait()
+
+    stores = []
+
+    def store(near, far):
+        c = pltpu.make_async_copy(near, far, out_sem.at[len(stores)])
+        c.start()
+        stores.append(c)
+
     barrier = pltpu.get_barrier_semaphore()
     for p in peers:
         pl.semaphore_signal(barrier, inc=1, device_id={"seq": p}, device_id_type=MESH)
     for z in zpeers:
         pl.semaphore_signal(barrier, inc=1, device_id={"chan": z}, device_id_type=MESH)
 
+    def gate_block(p):
+        at = lane(p)
+        su_send[p, 0] = (bk[:, at].astype(F32) * bv[:, at].astype(F32)).astype(BF16)
+        su_send[p, 1] = (bg[:, at].astype(F32) * bq[:, at].astype(F32)).astype(BF16)
+
+    loaded(filt)
     for h in range(per):
         fz[mz * per + h] = filt[:, h * w:(h + 1) * w].astype(BF16)
-    for p in range(n):
-        cols = slice(p * w, (p + 1) * w)
-        su_send[p, 0] = (bk[:, cols].astype(F32) * bv[:, cols].astype(F32)).astype(BF16)
-        su_send[p, 1] = (bg[:, cols].astype(F32) * bq[:, cols].astype(F32)).astype(BF16)
     pl.semaphore_wait(barrier, n - 1 + nc - 1)
-
     for z in zpeers:
         part = fz.at[pl.ds(mz * per, per)]
         send(part, part, z_ss.at[z], z_rs.at[mz], {"chan": z})
+    loaded(bk, bv, bg, bq)
     for p in peers:
+        gate_block(p)
         send(su_send.at[p], su.at[me], su_ss.at[p], su_rs.at[me], {"seq": p})
+    gate_block(me)
+    su[me] = su_send[me]
+    loaded(fk, fv)
     for p in range(n):
         cols = slice(p * w, (p + 1) * w)
         s1_send[p] = (fk[:, cols].astype(F32) * fv[:, cols].astype(F32)).astype(BF16)
+    s1[me] = s1_send[me]
+    loaded(fwd_t, inv_t)
     for z in zpeers:
         arrived(fz.at[pl.ds(z * per, per)], z_ss.at[z], z_rs.at[z], {"chan": z})
     for p in peers:
         send(fz.at[p], rf.at[me], f_ss.at[p], f_rs.at[me], {"seq": p})
     for p in peers:
         send(s1_send.at[p], s1.at[me], s1_ss.at[p], s1_rs.at[me], {"seq": p})
-    su[me] = su_send[me]
-    s1[me] = s1_send[me]
     rf[me] = fz[me]
 
     def transform(dst, q, block):
@@ -310,11 +335,10 @@
         return jnp.dot(inv_t[...], prod[b].astype(BF16), preferred_element_type=F32)
 
     def give_back(which):
-        for b in range(n):
-            c_send[which, b] = inverse(b).astype(BF16)
         for p in peers:
+            c_send[which, p] = inverse(p).astype(BF16)
             send(c_send.at[which, p], c_recv.at[which, me], c_ss.at[which, p], c_rs.at[which, me], {"seq": p})
-        c_recv[which, me] = c_send[which, me]
+        c_recv[which, me] = inverse(me).astype(BF16)
 
     total = jnp.zeros((1, w), F32)
     for q in [me] + peers:
@@ -330,11 +354,10 @@
 
     windowed(spec_s)
     products(spec_u, True)
-    for b in range(n):
-        g_send[b] = (inverse(b) * scale).astype(BF16)
     for p in peers:
+        g_send[p] = (inverse(p) * scale).astype(BF16)
         send(g_send.at[p], rg.at[me], g_ss.at[p], g_rs.at[me], {"seq": p})
-    rg[me] = g_send[me]
+    rg[me] = (inverse(me) * scale).astype(BF16)
 
     for q in [me] + peers:
         if q is not me:
@@ -358,6 +381,7 @@
     for z in zpeers:
         send(rg.at[pl.ds(z * per, per)], zg.at[mz], y_ss.at[z], y_rs.at[mz], {"chan": z})
 
+    loaded(skip, fq)
     for q in [me] + peers:
         at = lane(q)
         gain = skip[:, at]
@@ -365,6 +389,7 @@
             arrived(c_recv.at[0, q], c_ss.at[0, q], c_rs.at[0, q], {"seq": q})
         mixed = c_recv[0, q].astype(F32) + gain * su_send[q, 0].astype(F32)
         gq_o[:, at] = (bg[:, at].astype(F32) * mixed).astype(BF16)
+    store(gq_o, gq_h)
     for q in [me] + peers:
         at = lane(q)
         gain = skip[:, at]
@@ -373,6 +398,8 @@
         through = c_recv[1, q].astype(F32) + gain * su_send[q, 1].astype(F32)
         gk_o[:, at] = (through * bv[:, at].astype(F32)).astype(BF16)
         gv_o[:, at] = (through * bk[:, at].astype(F32)).astype(BF16)
+    store(gk_o, gk_h)
+    store(gv_o, gv_h)
     for z in zpeers:
         arrived(zg.at[z], y_ss.at[z], y_rs.at[z], {"chan": z})
     for h in range(per):
@@ -380,10 +407,12 @@
         for z in zpeers:
             acc += zg[z, h].astype(F32)
         gf_o[:, h * w:(h + 1) * w] = acc
+    store(gf_o, gf_h)
     for q in peers:
         arrived(k_recv.at[q], k_ss.at[q], k_rs.at[q], {"seq": q})
     for q in range(n):
         gs_o[:, q * w:(q + 1) * w] = k_recv[q, 0:1]
+    store(gs_o, gs_h)
     for q in [me] + peers:
         at = lane(q)
         gain = skip[:, at]
@@ -391,8 +420,26 @@
             arrived(c_recv.at[2, q], c_ss.at[2, q], c_rs.at[2, q], {"seq": q})
         mixed = c_recv[2, q].astype(F32) + gain * s1_send[q].astype(F32)
         out_o[:, at] = (fq[:, at].astype(F32) * mixed).astype(BF16)
+    store(out_o, out_h)
     for c in started:
         c.wait_send()
+    for c in stores:
+        c.wait()
+
+
+def store_all(*refs):
+    count = len(refs) // 3
+    far, out, near = refs[:count], refs[count:2 * count], refs[2 * count:-1]
+    sems = refs[-1]
+    loads = [pltpu.make_async_copy(far[i], near[i], sems.at[0, i]) for i in range(count)]
+    stores = [pltpu.make_async_copy(near[i], out[i], sems.at[1, i]) for i in range(count)]
+    for c in loads:
+        c.start()
+    for i in range(count):
+        loads[i].wait()
+        stores[i].start()
+    for c in stores:
+        c.wait()
 
 
 def fused_device(n, nc, *args):
@@ -403,11 +450,17 @@
     scale = 1.0 / math.sqrt(rows * n)
     forward, inverse = (jnp.asarray(t, dtype=BF16) for t in block_tables(rows))
     wide = jax.ShapeDtypeStruct((rows, chan_width), BF16)
-    vmem = pl.BlockSpec(memory_space=pltpu.VMEM)
+    results = [
+        *[pltpu.VMEM((rows, chan_width), BF16)] * 4, pltpu.VMEM(filters.shape, F32), pltpu.VMEM((1, chan_width), F32),
+    ]
     dma = pltpu.SemaphoreType.DMA
     block = (n, rows, w)
     spectrum = (n, 2 * rows, w)
     scratch = [
+        *[pltpu.VMEM((rows, chan_width), BF16)] * 7, pltpu.VMEM(filters.shape, F32),
+        pltpu.VMEM((1, chan_width), F32), pltpu.VMEM(forward.shape, BF16), pltpu.VMEM(inverse.shape, BF16),
+        dma((11,)),
+        *results, dma((6,)),
         pltpu.VMEM((n, 2, rows, w), BF16), pltpu.VMEM(block, BF16), pltpu.VMEM(block, BF16),
         pltpu.VMEM((n, 2, rows, w), BF16), pltpu.VMEM(block, BF16), pltpu.VMEM(block, BF16),
         *[pltpu.VMEM(spectrum, F32)] * 5,
@@ -417,20 +470,30 @@
         dma((n,)), dma((n,)), dma((n,)), dma((n,)), dma((n,)), dma((n,)), dma((nc,)), dma((nc,)),
         dma((3, n)), dma((3, n)), dma((n,)), dma((n,)), dma((nc,)), dma((nc,)), dma((n,)), dma((n,)),
     ]
+    full = 67_000_000
+    hbm = pl.BlockSpec(memory_space=pltpu.HBM)
     outs = pl.pallas_call(
         functools.partial(kernel, n, nc, scale),
         out_shape=(
             wide, wide, wide, wide,
             jax.ShapeDtypeStruct(filters.shape, F32), jax.ShapeDtypeStruct((1, chan_width), F32),
         ),
-        in_specs=[vmem] * 11,
-        out_specs=(vmem,) * 6,
+        in_specs=[hbm] * 11,
+        out_specs=(hbm,) * 6,
         scratch_shapes=scratch,
         compiler_params=pltpu.CompilerParams(
-            collective_id=0, has_side_effects=True, vmem_limit_bytes=48 * 1024 * 1024
+            collective_id=0, has_side_effects=True, vmem_limit_bytes=full
         ),
     )(*args[:8], skip.reshape(1, chan_width), forward, inverse)
-    return outs[:5] + (outs[5].reshape(chan_width),)
+    outs = pl.pallas_call(
+        store_all,
+        out_shape=tuple(jax.ShapeDtypeStruct(o.shape, o.dtype) for o in outs),
+        in_specs=[hbm] * 6,
+        out_specs=(hbm,) * 6,
+        scratch_shapes=[*results, dma((2, 6))],
+        compiler_params=pltpu.CompilerParams(vmem_limit_bytes=full),
+    )(*outs)
+    return tuple(outs[:5]) + (outs[5].reshape(chan_width),)
 
 
 def routed(*args):

time: 46.3 us -> 37 us (0.80)
  local copies, waits for them, and re-layouts: 14 us -> 0 us
  Pallas kernels: 31.2 us -> 36.2 us
    unnamed x28 -> x0, local copies, waits for them, and re-layouts: 14 us -> none
    pallas_call x1, Pallas kernels: 31.2 us -> 34.1 us  [fused_device(): pl.pallas_call(functools.partial(kernel, n, nc, scale), out_shape=(wide,...]
    pallas_call x0 -> x1, Pallas kernels: none -> 2.06 us  [fused_device(): pl.pallas_call(store_all, out_shape=tuple((jax.ShapeDtypeStruct(o.shape,...]
where the time goes in v1:
time: 37 us; the launch traced here: 36.8 us
  Pallas kernels  36.2 us (98%)
  between operations  0.64 us (2%)
    pallas_call x1, Pallas kernels, fused_device(): pl.pallas_call(functools.partial(kernel, n, nc, scale), out_shape=(wide,...  34.1 us
    pallas_call x1, Pallas kernels, fused_device(): pl.pallas_call(store_all, out_shape=tuple((jax.ShapeDtypeStruct(o.shape,...  2.06 us

profile of v1, /device:TPU:0, one launch (start us, length us, event | category | flops | bytes accessed | tf_op | source)
XLA Modules:
  0.0 36.8 jit_solution(17182897766345059416)
XLA Ops:
  0.6 34.1 %shard_map.154 = (bf16[128,1024]{1,0:T(8,128)(2,1)}, bf16[128,1024]{1,0:T(8,128)(2,1)}, bf16[128,1024]{1,0:T(8,128)(2,1)}, bf16[128,1024]{1,0:T(8,128)(2,1)}, f32[128,256]{1,0:T(8,128)}, /*index=5*/f32[1,1024]{1,0:T(1,128)}) custom-call(bf16[128,1024]{1,0:T(8,128)(2,1)} %fq_h.1, bf16[128,1024]{1,0:T(8,128)(2,1)} %fk_h.1, bf16[128,1024]{1,0:T(8,128)(2,1)} %fv_h.1, ...), custom_call_target="tpu_custom_call" | custom-call | tf_op jit(solution)/shard_map/pallas_call | solution.py:475
  34.8 2.1 %shard_map.155 = (bf16[128,1024]{1,0:T(8,128)(2,1)}, bf16[128,1024]{1,0:T(8,128)(2,1)}, bf16[128,1024]{1,0:T(8,128)(2,1)}, bf16[128,1024]{1,0:T(8,128)(2,1)}, f32[128,256]{1,0:T(8,128)}, /*index=5*/f32[1,1024]{1,0:T(1,128)}) custom-call(bf16[128,1024]{1,0:T(8,128)(2,1)} %get-tuple-element.18.refs_0_, bf16[128,1024]{1,0:T(8,128)(2,1)} %get-tuple-element.19.refs_1_, ...), custom_call_target="tpu_custom_call" | custom-call | tf_op jit(solution)/shard_map/pallas_call | solution.py:488

commit v2 on v1

--- a/solution.py
+++ b/solution.py
@@ -211,12 +211,13 @@
     fq, fk, fv, bq, bk, bv, bg, filt, skip, fwd_t, inv_t, in_sem,
     out_o, gq_o, gk_o, gv_o, gf_o, gs_o, out_sem,
     su_send, s1_send, fz, su, s1, rf, spec_s, spec_u, spec_f, spec_w, prod,
-    c_send, c_recv, g_send, rg, zg, k_send, k_recv,
-    su_ss, su_rs, s1_ss, s1_rs, f_ss, f_rs, z_ss, z_rs, c_ss, c_rs, g_ss, g_rs, y_ss, y_rs, k_ss, k_rs,
+    c_send, c_recv, g_send, g_recv, g_sum, rg, zg, k_send, k_recv,
+    su_ss, su_rs, s1_ss, s1_rs, f_ss, f_rs, z_ss, z_rs, c_ss, c_rs, g_ss, g_rs, y_ss, y_rs, k_ss, k_rs, x_ss, x_rs,
 ):
     rows, chan_width = fq.shape
     w = chan_width // n
     per = filt.shape[1] // w
+    part_rows = rows // nc
     me = lax.axis_index("seq")
     mz = lax.axis_index("chan")
     peers = [lax.rem(me + r, n) for r in range(1, n)]
@@ -261,6 +262,9 @@
         pl.semaphore_signal(barrier, inc=1, device_id={"seq": p}, device_id_type=MESH)
     for z in zpeers:
         pl.semaphore_signal(barrier, inc=1, device_id={"chan": z}, device_id_type=MESH)
+
+    def transform(dst, q, block):
+        dst[q] = jnp.dot(fwd_t[...], block, preferred_element_type=F32)
 
     def gate_block(p):
         at = lane(p)
@@ -286,6 +290,8 @@
         s1_send[p] = (fk[:, cols].astype(F32) * fv[:, cols].astype(F32)).astype(BF16)
     s1[me] = s1_send[me]
     loaded(fwd_t, inv_t)
+    transform(spec_s, me, su[me, 0])
+    transform(spec_u, me, su[me, 1])
     for z in zpeers:
         arrived(fz.at[pl.ds(z * per, per)], z_ss.at[z], z_rs.at[z], {"chan": z})
     for p in peers:
@@ -293,9 +299,6 @@
     for p in peers:
         send(s1_send.at[p], s1.at[me], s1_ss.at[p], s1_rs.at[me], {"seq": p})
     rf[me] = fz[me]
-
-    def transform(dst, q, block):
-        dst[q] = jnp.dot(fwd_t[...], block, preferred_element_type=F32)
 
     sign = 1.0 - 2.0 * lax.rem(lax.broadcasted_iota(jnp.int32, (rows, w), 0), 2).astype(F32)
 
@@ -344,8 +347,8 @@
     for q in [me] + peers:
         if q is not me:
             arrived(su.at[q], su_ss.at[q], su_rs.at[q], {"seq": q})
-        transform(spec_s, q, su[q, 0])
-        transform(spec_u, q, su[q, 1])
+            transform(spec_s, q, su[q, 0])
+            transform(spec_u, q, su[q, 1])
         total += jnp.sum(su[q, 0].astype(F32) * su[q, 1].astype(F32), axis=0, keepdims=True)
     k_send[...] = jnp.broadcast_to(total * scale, k_send.shape)
     for p in peers:
@@ -354,10 +357,12 @@
 
     windowed(spec_s)
     products(spec_u, True)
-    for p in peers:
-        g_send[p] = (inverse(p) * scale).astype(BF16)
-        send(g_send.at[p], rg.at[me], g_ss.at[p], g_rs.at[me], {"seq": p})
-    rg[me] = (inverse(me) * scale).astype(BF16)
+    for b in range(n):
+        term = (inverse(b) * scale).astype(BF16)
+        for z in range(nc):
+            g_send[z, b] = term[z * part_rows:(z + 1) * part_rows]
+    for z in zpeers:
+        send(g_send.at[z], g_recv.at[mz], x_ss.at[z], x_rs.at[mz], {"chan": z})
 
     for q in [me] + peers:
         if q is not me:
@@ -374,6 +379,15 @@
             arrived(s1.at[q], s1_ss.at[q], s1_rs.at[q], {"seq": q})
         transform(spec_s, q, s1[q])
     products(spec_s, False)
+    for z in zpeers:
+        arrived(g_recv.at[z], x_ss.at[z], x_rs.at[z], {"chan": z})
+    acc = g_send[mz].astype(F32)
+    for z in zpeers:
+        acc += g_recv[z].astype(F32)
+    g_sum[...] = acc.astype(BF16)
+    for p in peers:
+        send(g_sum.at[p], rg.at[me], g_ss.at[p], g_rs.at[me], {"seq": p})
+    rg[me] = g_sum[me]
     give_back(2)
 
     for q in peers:
@@ -402,11 +416,10 @@
     store(gv_o, gv_h)
     for z in zpeers:
         arrived(zg.at[z], y_ss.at[z], y_rs.at[z], {"chan": z})
-    for h in range(per):
-        acc = rg[mz * per + h].astype(F32)
-        for z in zpeers:
-            acc += zg[z, h].astype(F32)
-        gf_o[:, h * w:(h + 1) * w] = acc
+    zg[mz] = rg[pl.ds(mz * per, per)]
+    for z in range(nc):
+        for h in range(per):
+            gf_o[z * part_rows:(z + 1) * part_rows, h * w:(h + 1) * w] = zg[z, h].astype(F32)
     store(gf_o, gf_h)
     for q in peers:
         arrived(k_recv.at[q], k_ss.at[q], k_rs.at[q], {"seq": q})
@@ -455,6 +468,7 @@
     ]
     dma = pltpu.SemaphoreType.DMA
     block = (n, rows, w)
+    part = (n, rows // nc, w)
     spectrum = (n, 2 * rows, w)
     scratch = [
         *[pltpu.VMEM((rows, chan_width), BF16)] * 7, pltpu.VMEM(filters.shape, F32),
@@ -465,10 +479,12 @@
         pltpu.VMEM((n, 2, rows, w), BF16), pltpu.VMEM(block, BF16), pltpu.VMEM(block, BF16),
         *[pltpu.VMEM(spectrum, F32)] * 5,
         pltpu.VMEM((3,) + block, BF16), pltpu.VMEM((3,) + block, BF16),
-        pltpu.VMEM(block, BF16), pltpu.VMEM(block, BF16), pltpu.VMEM((nc, per, rows, w), BF16),
+        pltpu.VMEM((nc,) + part, BF16), pltpu.VMEM((nc,) + part, BF16), pltpu.VMEM(part, BF16),
+        pltpu.VMEM(part, BF16), pltpu.VMEM((nc, per, rows // nc, w), BF16),
         pltpu.VMEM((8, w), F32), pltpu.VMEM((n, 8, w), F32),
         dma((n,)), dma((n,)), dma((n,)), dma((n,)), dma((n,)), dma((n,)), dma((nc,)), dma((nc,)),
         dma((3, n)), dma((3, n)), dma((n,)), dma((n,)), dma((nc,)), dma((nc,)), dma((n,)), dma((n,)),
+        dma((nc,)), dma((nc,)),
     ]
     full = 67_000_000
     hbm = pl.BlockSpec(memory_space=pltpu.HBM)
@@ -500,7 +516,7 @@
     n, nc = lax.axis_size("seq"), lax.axis_size("chan")
     rows, chan_width = args[0].shape
     filter_width = args[7].shape[1]
-    fits = chan_width % (n * LANES) == 0 and rows % 16 == 0
+    fits = chan_width % (n * LANES) == 0 and rows % (16 * nc) == 0
     if fits and filter_width * nc == chan_width and filter_width % (chan_width // n) == 0:
         return fused_device(n, nc, *args)
     return per_device(*args)

time: 37 us -> 37.9 us (1.024)
  Pallas kernels: 36.2 us -> 37.1 us
    pallas_call x1, Pallas kernels: 34.1 us -> 35 us  [fused_device(): pl.pallas_call(functools.partial(kernel, n, nc, scale), out_shape=(wide,...]
where the time goes in v2:
time: 37.9 us; the launch traced here: 37.7 us
  Pallas kernels  37.1 us (98%)
  between operations  0.64 us (2%)
    pallas_call x1, Pallas kernels, fused_device(): pl.pallas_call(functools.partial(kernel, n, nc, scale), out_shape=(wide,...  35 us
    pallas_call x1, Pallas kernels, fused_device(): pl.pallas_call(store_all, out_shape=tuple((jax.ShapeDtypeStruct(o.shape,...  2.06 us

profile of v2, /device:TPU:0, one launch (start us, length us, event | category | flops | bytes accessed | tf_op | source)
XLA Modules:
  0.0 37.7 jit_solution(6099018218884814483)
XLA Ops:
  0.6 35.0 %shard_map.154 = (bf16[128,1024]{1,0:T(8,128)(2,1)}, bf16[128,1024]{1,0:T(8,128)(2,1)}, bf16[128,1024]{1,0:T(8,128)(2,1)}, bf16[128,1024]{1,0:T(8,128)(2,1)}, f32[128,256]{1,0:T(8,128)}, /*index=5*/f32[1,1024]{1,0:T(1,128)}) custom-call(bf16[128,1024]{1,0:T(8,128)(2,1)} %fq_h.1, bf16[128,1024]{1,0:T(8,128)(2,1)} %fk_h.1, bf16[128,1024]{1,0:T(8,128)(2,1)} %fv_h.1, ...), custom_call_target="tpu_custom_call" | custom-call | tf_op jit(solution)/shard_map/pallas_call | solution.py:491
  35.7 2.1 %shard_map.155 = (bf16[128,1024]{1,0:T(8,128)(2,1)}, bf16[128,1024]{1,0:T(8,128)(2,1)}, bf16[128,1024]{1,0:T(8,128)(2,1)}, bf16[128,1024]{1,0:T(8,128)(2,1)}, f32[128,256]{1,0:T(8,128)}, /*index=5*/f32[1,1024]{1,0:T(1,128)}) custom-call(bf16[128,1024]{1,0:T(8,128)(2,1)} %get-tuple-element.18.refs_0_, bf16[128,1024]{1,0:T(8,128)(2,1)} %get-tuple-element.19.refs_1_, ...), custom_call_target="tpu_custom_call" | custom-call | tf_op jit(solution)/shard_map/pallas_call | solution.py:504

commit v3 on v1

--- a/solution.py
+++ b/solution.py
@@ -220,6 +220,7 @@
     me = lax.axis_index("seq")
     mz = lax.axis_index("chan")
     peers = [lax.rem(me + r, n) for r in range(1, n)]
+    senders = peers[::-1]
     zpeers = [lax.rem(mz + r, nc) for r in range(1, nc)]
     started = []
 
@@ -261,6 +262,9 @@
         pl.semaphore_signal(barrier, inc=1, device_id={"seq": p}, device_id_type=MESH)
     for z in zpeers:
         pl.semaphore_signal(barrier, inc=1, device_id={"chan": z}, device_id_type=MESH)
+
+    def transform(dst, q, block):
+        dst[q] = jnp.dot(fwd_t[...], block, preferred_element_type=F32)
 
     def gate_block(p):
         at = lane(p)
@@ -286,6 +290,8 @@
         s1_send[p] = (fk[:, cols].astype(F32) * fv[:, cols].astype(F32)).astype(BF16)
     s1[me] = s1_send[me]
     loaded(fwd_t, inv_t)
+    transform(spec_s, me, su[me, 0])
+    transform(spec_u, me, su[me, 1])
     for z in zpeers:
         arrived(fz.at[pl.ds(z * per, per)], z_ss.at[z], z_rs.at[z], {"chan": z})
     for p in peers:
@@ -293,9 +299,6 @@
     for p in peers:
         send(s1_send.at[p], s1.at[me], s1_ss.at[p], s1_rs.at[me], {"seq": p})
     rf[me] = fz[me]
-
-    def transform(dst, q, block):
-        dst[q] = jnp.dot(fwd_t[...], block, preferred_element_type=F32)
 
     sign = 1.0 - 2.0 * lax.rem(lax.broadcasted_iota(jnp.int32, (rows, w), 0), 2).astype(F32)
 
@@ -341,11 +344,11 @@
         c_recv[which, me] = inverse(me).astype(BF16)
 
     total = jnp.zeros((1, w), F32)
-    for q in [me] + peers:
+    for q in [me] + senders:
         if q is not me:
             arrived(su.at[q], su_ss.at[q], su_rs.at[q], {"seq": q})
-        transform(spec_s, q, su[q, 0])
-        transform(spec_u, q, su[q, 1])
+            transform(spec_s, q, su[q, 0])
+            transform(spec_u, q, su[q, 1])
         total += jnp.sum(su[q, 0].astype(F32) * su[q, 1].astype(F32), axis=0, keepdims=True)
     k_send[...] = jnp.broadcast_to(total * scale, k_send.shape)
     for p in peers:
@@ -359,7 +362,7 @@
         send(g_send.at[p], rg.at[me], g_ss.at[p], g_rs.at[me], {"seq": p})
     rg[me] = (inverse(me) * scale).astype(BF16)
 
-    for q in [me] + peers:
+    for q in [me] + senders:
         if q is not me:
             arrived(rf.at[q], f_ss.at[q], f_rs.at[q], {"seq": q})
         transform(spec_f, q, rf[q])
@@ -369,20 +372,20 @@
     products(spec_u, True)
     give_back(1)
 
-    for q in [me] + peers:
+    for q in [me] + senders:
         if q is not me:
             arrived(s1.at[q], s1_ss.at[q], s1_rs.at[q], {"seq": q})
         transform(spec_s, q, s1[q])
     products(spec_s, False)
     give_back(2)
 
-    for q in peers:
+    for q in senders:
         arrived(rg.at[q], g_ss.at[q], g_rs.at[q], {"seq": q})
     for z in zpeers:
         send(rg.at[pl.ds(z * per, per)], zg.at[mz], y_ss.at[z], y_rs.at[mz], {"chan": z})
 
     loaded(skip, fq)
-    for q in [me] + peers:
+    for q in [me] + senders:
         at = lane(q)
         gain = skip[:, at]
         if q is not me:
@@ -390,7 +393,7 @@
         mixed = c_recv[0, q].astype(F32) + gain * su_send[q, 0].astype(F32)
         gq_o[:, at] = (bg[:, at].astype(F32) * mixed).astype(BF16)
     store(gq_o, gq_h)
-    for q in [me] + peers:
+    for q in [me] + senders:
         at = lane(q)
         gain = skip[:, at]
         if q is not me:
@@ -408,12 +411,12 @@
             acc += zg[z, h].astype(F32)
         gf_o[:, h * w:(h + 1) * w] = acc
     store(gf_o, gf_h)
-    for q in peers:
+    for q in senders:
         arrived(k_recv.at[q], k_ss.at[q], k_rs.at[q], {"seq": q})
     for q in range(n):
         gs_o[:, q * w:(q + 1) * w] = k_recv[q, 0:1]
     store(gs_o, gs_h)
-    for q in [me] + peers:
+    for q in [me] + senders:
         at = lane(q)
         gain = skip[:, at]
         if q is not me:

time: 37 us -> 36.9 us (level)
  no operation moved by 1% of the time
where the time goes in v3:
time: 36.9 us; the launch traced here: 36.7 us
  Pallas kernels  36.1 us (98%)
  between operations  0.64 us (2%)
    pallas_call x1, Pallas kernels, fused_device(): pl.pallas_call(functools.partial(kernel, n, nc, scale), out_shape=(wide,...  34 us
    pallas_call x1, Pallas kernels, fused_device(): pl.pallas_call(store_all, out_shape=tuple((jax.ShapeDtypeStruct(o.shape,...  2.06 us

profile of v3, /device:TPU:0, one launch (start us, length us, event | category | flops | bytes accessed | tf_op | source)
XLA Modules:
  0.0 36.7 jit_solution(7205605513673105369)
XLA Ops:
  0.6 34.0 %shard_map.154 = (bf16[128,1024]{1,0:T(8,128)(2,1)}, bf16[128,1024]{1,0:T(8,128)(2,1)}, bf16[128,1024]{1,0:T(8,128)(2,1)}, bf16[128,1024]{1,0:T(8,128)(2,1)}, f32[128,256]{1,0:T(8,128)}, /*index=5*/f32[1,1024]{1,0:T(1,128)}) custom-call(bf16[128,1024]{1,0:T(8,128)(2,1)} %fq_h.1, bf16[128,1024]{1,0:T(8,128)(2,1)} %fk_h.1, bf16[128,1024]{1,0:T(8,128)(2,1)} %fv_h.1, ...), custom_call_target="tpu_custom_call" | custom-call | tf_op jit(solution)/shard_map/pallas_call | solution.py:478
  34.7 2.1 %shard_map.155 = (bf16[128,1024]{1,0:T(8,128)(2,1)}, bf16[128,1024]{1,0:T(8,128)(2,1)}, bf16[128,1024]{1,0:T(8,128)(2,1)}, bf16[128,1024]{1,0:T(8,128)(2,1)}, f32[128,256]{1,0:T(8,128)}, /*index=5*/f32[1,1024]{1,0:T(1,128)}) custom-call(bf16[128,1024]{1,0:T(8,128)(2,1)} %get-tuple-element.18.refs_0_, bf16[128,1024]{1,0:T(8,128)(2,1)} %get-tuple-element.19.refs_1_, ...), custom_call_target="tpu_custom_call" | custom-call | tf_op jit(solution)/shard_map/pallas_call | solution.py:491
